TPU v7x, 32 devices: a whole 2x2x4 slice. The times are simulated.
32 devices in a mesh: lat: 16 (over z, y, x), fld: 2 (over core).
Axes of the slice: x: 2, y: 2, z: 4, core: 2. Of those that a mesh axis runs over, the one named last changes fastest.
Arguments:
- grid: bfloat16 [2, 4, 69, 640, 1408], P('fld', None, None, 'lat'), may hold values from -6 to 6
- cycle_ids: int32 [640], replicated, may hold values from 0 to 639, each once
- cycle_len: int32 [640], replicated, may hold values from 20 to 1296, as said below
- wave_ids: int32 [320], replicated, may hold values from 0 to 319, each once
- legendre: bfloat16 [320, 320, 640], P('lat'), may hold values from -0.25 to 0.25
- target: float32 [2, 4, 69, 2, 320, 320], P('fld', None, None, None, 'lat'), may hold values from -18 to 18
- step_w: float32 [2], P('fld'), may hold values from 0.5 to 2
- chan_w: float32 [69], replicated, may hold values from 0.2 to 2
Outputs:
- coeffs: float32 [2, 4, 69, 2, 320, 320], P('fld', None, None, None, 'lat')
- loss: float32 [], replicated
- field_grad: bfloat16 [2, 4, 69, 640, 1408], P('fld', None, None, 'lat')
Inputs may be any that keep to these rules, and one draw needn't show every extreme that they name: `cycle_len`: every length 20 + 4 j with j from 0 to 319 occurs exactly twice.
All inputs are finite; a program needn't handle non-finite values.
Results may differ from a plain program's by a relative error of at most 0.0065.
Values may be sent and summed in bfloat16 or wider, within the bound.
A program may use at most 320 MiB of HBM per device.

v0:
```python
import math

import jax
import jax.numpy as jnp
from jax import lax
from jax.sharding import PartitionSpec as P

STEPS = 2


def sin_cos(length, product):
    inverse = 1.0 / length.astype(jnp.float32)
    quarter = jnp.floor(product.astype(jnp.float32) * (4.0 * inverse) + 0.5).astype(jnp.int32)
    rest = 4 * product - quarter * length
    x = rest.astype(jnp.float32) * ((0.5 * math.pi) * inverse)
    x2 = x * x
    sin_x = x + x * x2 * (
        -1.0 / 6 + x2 * (1.0 / 120 + x2 * (-1.0 / 5040 + x2 * (1.0 / 362880)))
    )
    cos_x = 1.0 + x2 * (
        -0.5 + x2 * (1.0 / 24 + x2 * (-1.0 / 720 + x2 * (1.0 / 40320 - x2 * (1.0 / 3628800))))
    )
    odd = (quarter & 1) == 1
    sine = jnp.where(odd, cos_x, sin_x)
    cosine = jnp.where(odd, sin_x, cos_x)
    sine = jnp.where((quarter & 2) == 2, -sine, sine)
    cosine = jnp.where(((quarter + 1) & 2) == 2, -cosine, cosine)
    return sine, cosine


def cycle_tables(lengths, waves, is_sine, segment):
    inner = math.gcd(segment, 32)
    outer = segment // inner
    length = lengths[:, None, None]
    wave = waves[None, None, :]
    coarse = (inner * jnp.arange(outer, dtype=jnp.int32))[None, :, None]
    fine = jnp.arange(inner, dtype=jnp.int32)[None, :, None]
    sin_a, cos_a = sin_cos(length, wave * coarse)
    sin_b, cos_b = sin_cos(length, wave * fine)
    scale = jnp.where(2 * wave < length, lax.rsqrt(length.astype(jnp.float32)), 0.0)
    sine = is_sine[None, None, :]
    first = jnp.where(sine, -sin_a, cos_a) * scale
    second = jnp.where(sine, -cos_a, -sin_a) * scale
    first, second, sin_b, cos_b = lax.optimization_barrier((first, second, sin_b, cos_b))
    table = first[:, :, None, :] * cos_b[:, None, :, :] + second[:, :, None, :] * sin_b[:, None, :, :]
    inside = (coarse[..., None] + fine[:, None]) < length[..., None]
    table = jnp.where(inside, table, 0.0).astype(jnp.bfloat16)
    return table.reshape(lengths.shape[0], segment, waves.shape[0])


def per_device(lat, grid, cycle_ids, cycle_len, wave_ids, legendre, target, step_w, chan_w):
    _, batch_size, chan_count, cycle_dev, segment = grid.shape
    wave_count = wave_ids.shape[0]
    wave_dev, degrees, cycle_count = legendre.shape
    col_count = batch_size * chan_count
    lat_index = lax.axis_index("lat")
    my_cycles = lax.dynamic_slice_in_dim(cycle_ids, lat_index * cycle_dev, cycle_dev)
    lengths = jnp.take(cycle_len, my_cycles)

    pair = 2 * wave_dev
    by_owner = wave_ids.reshape(lat, 1, wave_dev)
    column_waves = jnp.broadcast_to(by_owner, (lat, 2, wave_dev)).reshape(-1)
    is_sine = (jnp.arange(lat * pair, dtype=jnp.int32) // wave_dev) % 2 == 1
    tables = cycle_tables(lengths, column_waves, is_sine, segment)
    tables = lax.optimization_barrier(tables)

    rows = grid[0].reshape(col_count, cycle_dev, segment)
    fourier = jnp.einsum("rkj,brk->rjb", tables, rows, preferred_element_type=jnp.float32)
    fourier = fourier.astype(jnp.bfloat16).reshape(cycle_dev, lat, pair, col_count)
    fourier = jnp.transpose(fourier, (1, 0, 2, 3))
    gathered = lax.all_to_all(fourier, "lat", split_axis=0, concat_axis=0, tiled=True)
    gathered = gathered.reshape(cycle_count, 2, wave_dev, col_count)

    legendre_cols = jnp.take(legendre, cycle_ids, axis=2)
    my_waves = lax.dynamic_slice_in_dim(wave_ids, lat_index * wave_dev, wave_dev)
    kept = jnp.arange(degrees, dtype=jnp.int32)[None, :] >= my_waves[:, None]
    kept = kept.astype(jnp.float32)[:, None, None, :]
    factor = jnp.where(my_waves == 0, 1.0, 2.0).astype(jnp.float32)
    weight_cols = jnp.broadcast_to(step_w[0] * chan_w[None, :], (batch_size, chan_count))
    weight = factor[:, None, None, None] * weight_cols.reshape(1, 1, col_count, 1)
    target_local = jnp.transpose(
        target[0].reshape(col_count, 2, wave_dev, degrees), (2, 1, 0, 3)
    )
    coeffs = jnp.einsum(
        "rpsb,snr->spbn", gathered, legendre_cols, preferred_element_type=jnp.float32
    )
    coeffs = coeffs * kept
    misfit = (coeffs - target_local) * kept
    partial_value = jnp.sum(weight * misfit * misfit)
    grad_coeff = (2.0 * weight * misfit).astype(jnp.bfloat16)
    back = jnp.einsum(
        "snr,spbn->sprb", legendre_cols, grad_coeff, preferred_element_type=jnp.float32
    )
    back = jnp.transpose(back.astype(jnp.bfloat16), (2, 1, 0, 3))
    back = back.reshape(lat, cycle_dev, pair, col_count)
    returned = lax.all_to_all(back, "lat", split_axis=0, concat_axis=0, tiled=True)
    returned = jnp.transpose(returned, (1, 0, 2, 3)).reshape(cycle_dev, lat * pair, col_count)
    field = jnp.einsum("rjb,rkj->brk", returned, tables, preferred_element_type=jnp.float32)
    field_grad = field.astype(jnp.bfloat16).reshape(
        1, batch_size, chan_count, cycle_dev, segment
    )
    coeff_out = jnp.transpose(coeffs, (2, 1, 0, 3)).reshape(
        1, batch_size, chan_count, 2, wave_dev, degrees
    )
    loss_sum = lax.psum(partial_value, ("lat", "fld"))
    term_count = STEPS * col_count * wave_count * (wave_count + 1) // 2
    loss = loss_sum / jnp.float32(term_count)
    return (coeff_out, loss, field_grad)


def solution(mesh):
    lat = mesh.shape["lat"]
    return jax.shard_map(
        lambda *args: per_device(lat, *args),
        mesh=mesh,
        in_specs=(
            P("fld", None, None, "lat", None),
            P(),
            P(),
            P(),
            P("lat", None, None),
            P("fld", None, None, None, "lat", None),
            P("fld"),
            P(),
        ),
        out_specs=(P("fld", None, None, None, "lat", None), P(), P("fld", None, None, "lat", None)),
        check_vma=False,
    )
```

profile of v0, /device:TPU:0, one launch (start us, length us, event | category | flops | bytes accessed | tf_op | source)
XLA Modules:
  0.0 1336.6 jit_solution(13408419397159870549)
XLA Ops:
  4.8 6.8 negate_select_fusion.2
  11.6 9.4 select_multiply_fusion
  21.3 34.2 %multiply_add_fusion = bf16[40,44,32,640]{3,2,1,0:T(8,128)(2,1)} fusion(f32[40,32,640]{2,1,0:T(8,128)} %get-tuple-element.10, f32[40,44,640]{2,1,0:T(8,128)} %get-tuple-element.9, f32[40,32,640]{2,1,0:T(8,128)S(1)} %get-tuple-element.8, f32[40,44,640]{2,1,0:T(8,128)} %get-tuple-element.7), kind=kLoop, calls=%fused_computation.4 | loop fusion | flops 144179200 | bytes 87654400 | tf_op jit(solution)/shard_map/add | solution.py:45
  55.5 47.6 %fusion = bf16[40,1408,640]{2,1,0:T(8,128)(2,1)} fusion(bf16[40,44,32,640]{3,2,1,0:T(8,128)(2,1)} %multiply_add_fusion, pred[40,1408]{1,0:T(8,128)(4,1)S(1)} %broadcast_compare_fusion), kind=kLoop, calls=%fused_computation.3 | loop fusion | flops 36044800 | bytes 144235520 | tf_op jit(solution)/shard_map/convert_element_type | solution.py:47
  103.1 45.3 %fusion.8 = bf16[40,640,276]{1,2,0:T(8,128)(2,1)} fusion(bf16[40,1408,640]{2,1,0:T(8,128)(2,1)} %fusion, bf16[276,40,1408]{2,1,0:T(8,128)(2,1)} %bitcast.49), kind=kOutput, calls=%fused_computation.19 | convolution fusion | flops 19903795200 | bytes 117309440 | tf_op jit(solution)/shard_map/rkj,brk->rjb/dot_general | solution.py:68
  148.4 22.3 %copy.29 = bf16[40,640,276]{2,1,0:T(8,128)(2,1)} copy(bf16[40,640,276]{1,2,0:T(8,128)(2,1)} %fusion.8) | data formatting | bytes 28262400 | tf_op jit(solution)/shard_map/convert_element_type | solution.py:69
  170.7 17.1 %copy.30 = bf16[16,40,40,276]{3,2,1,0:T(8,128)(2,1)} copy(bf16[16,40,40,276]{3,2,0,1:T(8,128)(2,1)} %bitcast.42) | data formatting | bytes 28262400 | tf_op jit(solution)/shard_map/transpose | solution.py:70
  187.8 8.6 all-to-all-start
  196.4 15.0 %copy.32 = bf16[20,320,640]{1,0,2:T(8,128)(2,1)} copy(bf16[20,320,640]{2,1,0:T(8,128)(2,1)} %param.12) | data formatting | bytes 16384000 | tf_op args[4]
  211.4 25.5 %gather_fusion.1 = bf16[640,20,320]{2,1,0:T(8,128)(2,1)} fusion(bf16[20,320,640]{1,0,2:T(8,128)(2,1)} %copy.32, s32[1024]{0:T(1024)S(1)} %pad_clamp_fusion), kind=kCustom, calls=%fused_computation.1 | custom fusion | bytes 16386560 | tf_op jit(solution)/shard_map/jit(_take)/gather | solution.py:74
  236.9 11.0 select_bitcast_fusion
  247.9 14.9 %copy.44 = bf16[20,320,640,1]{2,1,3,0:T(8,128)(2,1)} copy(bf16[20,320,640,1]{1,0,2,3:T(8,128)(2,1)} %select_bitcast_fusion) | data formatting | bytes 16384000 | tf_op jit(solution)/shard_map/jit(_take)/select_n | solution.py:74
  264.5 300.9 %all-to-all-done = bf16[16,40,40,276]{3,2,1,0:T(8,128)(2,1)} async-done(((bf16[16,40,40,276]{3,2,1,0:T(8,128)(2,1)}), bf16[16,40,40,276]{3,2,1,0:T(8,128)(2,1)}, u32[]{:S(2)}, u32[]{:S(2)}) %all-to-all-start) | async-done | bytes 14131232 | tf_op jit(solution)/shard_map/all_to_all | solution.py:71
  565.4 18.6 %copy.31 = bf16[16,40,40,276]{3,1,0,2:T(8,128)(2,1)} copy(bf16[16,40,40,276]{3,2,1,0:T(8,128)(2,1)} %all-to-all-done) | data formatting | bytes 28262400 | tf_op jit(solution)/shard_map/all_to_all | solution.py:71
  584.0 18.1 %fusion.4 = f32[20,2,276,320]{3,2,1,0:T(8,128)} fusion(bf16[20,320,640,1]{2,1,3,0:T(8,128)(2,1)S(1)} %copy-done.2, bf16[640,2,20,276]{3,0,2,1:T(8,128)(2,1)} %bitcast.47), kind=kOutput, calls=%fused_computation.10 | convolution fusion | flops 4521984000 | bytes 36454400 | tf_op jit(solution)/shard_map/rpsb,snr->spbn/dot_general | solution.py:84
  602.1 23.3 %convert_bitcast_fusion.1 = bf16[640,2,20,276]{0,3,1,2:T(8,128)(2,1)} fusion(bf16[20,320,640,1]{2,1,3,0:T(8,128)(2,1)} %copy.44, f32[20,276]{1,0:T(8,128)S(1)} %get-tuple-element.29, f32[276,2,20,320]{3,1,2,0:T(2,128)} %bitcast.44, f32[20,2,276,320]{3,2,1,0:T(8,128)} %fusion.4, f32[20,320]{1,0:T(8,128)S(1)} %fusion.36), kind=kOutput, calls=%fused_computation.17 | convolution fusion | flops 4546713600 | bytes 50633280 | tf_op jit(solution)/shard_map/snr,spbn->sprb/dot_general | solution.py:91
  625.5 22.3 %copy.38 = bf16[640,2,20,276]{3,0,2,1:T(8,128)(2,1)} copy(bf16[640,2,20,276]{0,3,1,2:T(8,128)(2,1)} %convert_bitcast_fusion.1) | data formatting | bytes 28262400 | tf_op jit(solution)/shard_map/convert_element_type | solution.py:94
  647.8 17.0 %copy.39 = bf16[16,40,40,276]{3,1,2,0:T(8,128)(2,1)} copy(bf16[16,40,40,276]{3,1,0,2:T(8,128)(2,1)} %bitcast.43) | data formatting | bytes 28262400 | tf_op jit(solution)/shard_map/reshape | solution.py:95
  664.8 86.3 %all-to-all-start.1 = ((bf16[16,40,40,276]{3,1,2,0:T(8,128)(2,1)}), bf16[16,40,40,276]{3,1,2,0:T(8,128)(2,1)}, u32[]{:S(2)}, u32[]{:S(2)}) async-start(bf16[16,40,40,276]{3,1,2,0:T(8,128)(2,1)} %copy.39), calls=%async_computation.1 | async-start | bytes 39321600 | tf_op jit(solution)/shard_map/all_to_all | solution.py:96
  751.1 18.9 %fusion.6 = (f32[]{:T(128)}, f32[276,2,20,320]{3,0,1,2:T(8,128)}) fusion(f32[20,276]{1,0:T(8,128)S(1)} %get-tuple-element.30, f32[276,2,20,320]{3,1,2,0:T(2,128)} %bitcast.45, f32[20,2,276,320]{3,2,1,0:T(8,128)} %fusion.4, f32[20,320]{1,0:T(8,128)S(1)} %fusion.36), kind=kLoop, calls=%fused_computation.12 | loop fusion | flops 21196800 | bytes 42441284 | tf_op jit(solution)/shard_map/reduce_sum | solution.py:89
  770.0 447.4 %psum.7 = f32[]{:T(128)} all-reduce(f32[]{:T(128)} %get-tuple-element.19), channel_id=1, replica_groups=mesh['lat'=16,'fld'=2] {'lat','fld'}, use_global_device_ids=true, to_apply=%region_1.2 | all-reduce | flops 1 | bytes 8 | tf_op jit(solution)/shard_map/psum | solution.py:105
  1217.4 30.0 %copy.35 = f32[276,2,20,320]{3,1,2,0:T(2,128)} copy(f32[276,2,20,320]{3,0,1,2:T(8,128)} %get-tuple-element.20) | data formatting | bytes 28262400 | tf_op jit(solution)/shard_map/mul | solution.py:87
  1248.1 51.3 %convert_bitcast_fusion = bf16[276,40,1408]{2,0,1:T(8,128)(2,1)} fusion(bf16[40,1408,640]{2,1,0:T(8,128)(2,1)} %fusion, bf16[40,640,276]{2,0,1:T(8,128)(2,1)} %bitcast.16), kind=kOutput, calls=%fused_computation.7 | convolution fusion | flops 19912273920 | bytes 117309440 | tf_op jit(solution)/shard_map/rjb,rkj->brk/dot_general | solution.py:98
  1299.4 35.6 %copy.42 = bf16[276,40,1408]{2,1,0:T(8,128)(2,1)} copy(bf16[276,40,1408]{2,0,1:T(8,128)(2,1)} %convert_bitcast_fusion) | data formatting | bytes 62177280 | tf_op jit(solution)/shard_map/convert_element_type | solution.py:99
  (37 shorter events, 5.3 us)
Async XLA Ops:
  0.6 2.6 copy-start
  187.8 377.6 %all-to-all-start = ((bf16[16,40,40,276]{3,2,1,0:T(8,128)(2,1)}), bf16[16,40,40,276]{3,2,1,0:T(8,128)(2,1)}, u32[]{:S(2)}, u32[]{:S(2)}) async-start(bf16[16,40,40,276]{3,2,1,0:T(8,128)(2,1)} %copy.30), calls=%async_computation | async-start | bytes 39321600 | tf_op jit(solution)/shard_map/all_to_all | solution.py:71
  196.4 15.0 %copy-start.3 = (s32[640]{0:T(1024)S(1)}, s32[640]{0:T(1024)}, u32[]{:S(2)}) copy-start(s32[640]{0:T(1024)} %param.9) | copy-start | bytes 7684
  247.9 15.5 %copy-start.4 = (f32[69]{0:T(128)S(1)}, f32[69]{0:T(128)}, u32[]{:S(2)}) copy-start(f32[69]{0:T(128)} %param.15) | copy-start | bytes 832
  565.4 18.6 %copy-start.2 = (bf16[20,320,640,1]{2,1,3,0:T(8,128)(2,1)S(1)}, bf16[20,320,640,1]{2,1,3,0:T(8,128)(2,1)}, u32[]{:S(2)}) copy-start(bf16[20,320,640,1]{2,1,3,0:T(8,128)(2,1)} %copy.44) | copy-start | bytes 24576004
  664.8 583.3 %all-to-all-start.1 = ((bf16[16,40,40,276]{3,1,2,0:T(8,128)(2,1)}), bf16[16,40,40,276]{3,1,2,0:T(8,128)(2,1)}, u32[]{:S(2)}, u32[]{:S(2)}) async-start(bf16[16,40,40,276]{3,1,2,0:T(8,128)(2,1)} %copy.39), calls=%async_computation.1 | async-start | bytes 39321600 | tf_op jit(solution)/shard_map/all_to_all | solution.py:96
  1299.4 35.6 %copy-start.1 = (s32[640]{0:T(1024)S(1)}, s32[640]{0:T(1024)}, u32[]{:S(2)}) copy-start(s32[640]{0:T(1024)} %param.10) | copy-start | bytes 7684
where the time goes:
time: 1350 us; the launch traced here: 1340 us
  blocking collectives  447 us (33%)
  waiting for transfers between devices  301 us (22%)
  local copies, waits for them, and re-layouts  220 us (16%)
  matrix products  138 us (10%)
  other arithmetic  132 us (10%)
  starting transfers between devices  94.9 us (7%)
    psum x1, blocking collectives, per_device(): loss_sum = lax.psum(partial_value, ('lat', 'fld'))  447 us
    all_to_all x1, waiting for transfers between devices, per_device(): lax.all_to_all(fourier, 'lat', split_axis=0, concat_axis=0, tiled=True)  301 us
    all_to_all x1, starting transfers between devices, per_device(): lax.all_to_all(back, 'lat', split_axis=0, concat_axis=0, tiled=True)  86.3 us
    dot_general x1, matrix products, per_device(): jnp.einsum('rjb,rkj->brk', returned, tables, preferred_element_type=jnp.f...  51.3 us
    convert_element_type x1, other arithmetic, cycle_tables(): table = jnp.where(inside, table, 0.0).astype(jnp.bfloat16)  47.6 us
    dot_general x1, matrix products, per_device(): jnp.einsum('rkj,brk->rjb', tables, rows, preferred_element_type=jnp.float32)  45.3 us
    convert_element_type x1, local copies, waits for them, and re-layouts, per_device(): field.astype(jnp.bfloat16)  35.6 us
    add x1, other arithmetic, cycle_tables(): first[:, :, None, :] * cos_b[:, None, :, :]  34.2 us
  transfers between devices with their start and end apart: 2, of which 1 were waited for; matrix products, arithmetic and copies ran while one was open for 9% of the time, Pallas kernels for 0%

commit v1 on v0

--- a/solution.py
+++ b/solution.py
@@ -1,15 +1,25 @@
+import functools
 import math
 
 import jax
 import jax.numpy as jnp
 from jax import lax
+from jax.experimental import pallas as pl
+from jax.experimental.pallas import tpu as pltpu
 from jax.sharding import PartitionSpec as P
 
+
 STEPS = 2
-
-
-def sin_cos(length, product):
-    inverse = 1.0 / length.astype(jnp.float32)
+LANES = 128
+SUB = 8
+RUN = 64
+WAVES_STEP = 5
+PIECE = 24
+
+
+def sin_cos(length, product, inverse=None):
+    if inverse is None:
+        inverse = 1.0 / length.astype(jnp.float32)
     quarter = jnp.floor(product.astype(jnp.float32) * (4.0 * inverse) + 0.5).astype(jnp.int32)
     rest = 4 * product - quarter * length
     x = rest.astype(jnp.float32) * ((0.5 * math.pi) * inverse)
@@ -26,6 +36,438 @@
     sine = jnp.where((quarter & 2) == 2, -sine, sine)
     cosine = jnp.where(((quarter + 1) & 2) == 2, -cosine, cosine)
     return sine, cosine
+
+
+def make_table(length, inverse, root, wave_ref, sine_ref, table_ref):
+    segment, width = table_ref.shape
+
+    def lane_tile(tile, carry):
+        lanes = pl.ds(pl.multiple_of(tile * LANES, LANES), LANES)
+        wave = wave_ref[:, lanes]
+        is_sine = sine_ref[:, lanes] == 1
+        row = lax.broadcasted_iota(jnp.int32, (RUN, LANES), 0)
+        scale = jnp.where(2 * wave < length, root, 0.0)
+        sin_k, cos_k = sin_cos(length, row * wave, inverse)
+        sin_run, cos_run = sin_cos(length, RUN * wave, inverse)
+        before = jnp.where(is_sine, -sin_k, cos_k) * scale
+        slope = jnp.where(is_sine, -cos_k, -sin_k) * scale
+        now = before * cos_run + slope * sin_run
+        twice = 2.0 * cos_run
+        for step in range(segment // RUN):
+            value = jnp.where(row < length - step * RUN, before, 0.0)
+            table_ref[pl.ds(step * RUN, RUN), lanes] = value.astype(jnp.bfloat16)
+            before, now = now, twice * now - before
+        return carry
+
+    lax.fori_loop(0, width // LANES, lane_tile, 0)
+
+
+def forward_kernel(
+    lat, first, groups, len_ref, inv_ref, root_ref, wave_ref, sine_ref, grid_ref, *rest
+):
+    outs, (rows_ref, table_ref, flat_ref, main_ref, tail_ref) = rest[:-5], rest[-5:]
+    cols, _, segment = grid_ref.shape
+    width = table_ref.shape[1]
+    whole = cols // LANES * LANES
+    per_tile = 2 * WAVES_STEP // 2
+    block = pl.program_id(0) + first
+    chunk = 12 if cols % 12 == 0 else 1
+
+    def widen(i, carry):
+        part = grid_ref[pl.ds(i * chunk, chunk), :, :].astype(jnp.float32)
+        start = pl.multiple_of(i * chunk * SUB, SUB)
+        for t in range(segment // LANES):
+            piece = part[:, :, t * LANES : (t + 1) * LANES]
+            rows_ref[t, pl.ds(start, chunk * SUB), :] = piece.reshape(chunk * SUB, LANES)
+        return carry
+
+    lax.fori_loop(0, cols // chunk, widen, 0)
+    pad = flat_ref.shape[0]
+    flat_ref[cols // SUB * SUB :, :] = jnp.zeros((pad - cols // SUB * SUB, width), jnp.float32)
+
+    def cycle(r, carry):
+        slot = block * SUB + r
+        make_table(len_ref[slot], inv_ref[slot], root_ref[slot], wave_ref, sine_ref, table_ref)
+        rows = [
+            rows_ref[t, pl.ds(r, cols, stride=SUB), :].astype(jnp.bfloat16)
+            for t in range(segment // LANES)
+        ]
+        rows = jnp.concatenate(rows, axis=1)
+        flat_ref[:cols, :] = jnp.dot(rows, table_ref[...], preferred_element_type=jnp.float32)
+        for h in range(whole // LANES):
+            value = flat_ref[h * LANES : (h + 1) * LANES, :].T
+            main_ref[h, pl.ds(r, width, stride=SUB), :] = value
+        tail = flat_ref[whole:, :].T.reshape(width // lat, lat, LANES)
+        for t in range(width // lat // per_tile):
+            total = tail[t * per_tile]
+            for i in range(1, per_tile):
+                total = total + pltpu.roll(tail[t * per_tile + i], PIECE * i, axis=1)
+            tail_ref[pl.ds(t * lat * SUB + r, lat, stride=SUB), :] = total
+        return carry
+
+    lax.fori_loop(0, SUB, cycle, 0)
+
+    halves = whole // LANES
+    mains = 2 * WAVES_STEP * halves
+
+    def deliver(owner, carry):
+        quarter = 0
+        for out_ref, quarters in zip(outs, groups):
+            for q in range(quarters):
+                for jj in range(2 * WAVES_STEP):
+                    start = ((quarter * 2 * WAVES_STEP + jj) * lat + owner) * SUB
+                    for h in range(halves):
+                        piece = main_ref[h, pl.ds(pl.multiple_of(start, SUB), SUB), :]
+                        out_ref[owner, 0, q, jj * halves + h] = piece.astype(jnp.bfloat16)
+                for t in range(2):
+                    start = ((quarter * 2 + t) * lat + owner) * SUB
+                    value = tail_ref[pl.ds(pl.multiple_of(start, SUB), SUB), :]
+                    out_ref[owner, 0, q, mains + t] = value.astype(jnp.bfloat16)
+                quarter += 1
+        return carry
+
+    lax.fori_loop(0, lat, deliver, 0)
+
+
+def forward(lat, first, blocks, groups, lengths, inverse, root, waves, sine, rows):
+    cols, _, segment = rows.shape
+    width = waves.shape[1]
+    whole = cols // LANES * LANES
+    tiles = 2 * WAVES_STEP * (whole // LANES) + 2
+    smem = pl.BlockSpec(memory_space=pltpu.SMEM)
+    small = pl.BlockSpec((1, width), lambda b: (0, 0))
+    return pl.pallas_call(
+        functools.partial(forward_kernel, lat, first, groups),
+        grid=(blocks,),
+        in_specs=[smem, smem, smem, small, small]
+        + [pl.BlockSpec((cols, SUB, segment), lambda b: (0, b + first, 0))],
+        out_specs=[
+            pl.BlockSpec((lat, 1, q, tiles, SUB, LANES), lambda b: (0, b, 0, 0, 0, 0)) for q in groups
+        ],
+        out_shape=[
+            jax.ShapeDtypeStruct((lat, blocks, q, tiles, SUB, LANES), jnp.bfloat16) for q in groups
+        ],
+        scratch_shapes=[
+            pltpu.VMEM((segment // LANES, cols * SUB, LANES), jnp.float32),
+            pltpu.VMEM((segment, width), jnp.bfloat16),
+            pltpu.VMEM((whole + LANES, width), jnp.float32),
+            pltpu.VMEM((whole // LANES, width * SUB, LANES), jnp.float32),
+            pltpu.VMEM((width // WAVES_STEP * SUB, LANES), jnp.float32),
+        ],
+        compiler_params=pltpu.CompilerParams(vmem_limit_bytes=58 * 2**20),
+        cost_estimate=pl.CostEstimate(
+            flops=2 * cols * segment * width * SUB * blocks,
+            bytes_accessed=2 * cols * (segment + width) * SUB * blocks,
+            transcendentals=0,
+        ),
+        name="forward_cycles",
+    )(lengths, inverse, root, waves, sine, rows)
+
+
+def middle_kernel(lat, parts, wave_ref, weight_ref, legendre_ref, target_ref, *rest):
+    ins = rest[: len(parts[0])]
+    rest = rest[len(parts[0]) :]
+    coeff_ref, loss_ref = rest[:2]
+    outs, (grad_tail, flat_ref) = rest[2:-2], rest[-2:]
+    cols, degrees = weight_ref.shape
+    cycles = legendre_ref.shape[2]
+    whole = cols // LANES * LANES
+    halves = whole // LANES
+    mains = 2 * WAVES_STEP * halves
+    per_tile = WAVES_STEP
+    rows = lat * SUB
+    step = pl.program_id(0)
+    degree = lax.broadcasted_iota(jnp.int32, (cols, degrees), 1)
+
+    @pl.when(step == 0)
+    def _():
+        loss_ref[...] = jnp.zeros_like(loss_ref)
+
+    grad_tail[...] = jnp.zeros_like(grad_tail)
+    flat_ref[cols // SUB * SUB :, :] = jnp.zeros(
+        (flat_ref.shape[0] - cols // SUB * SUB, cycles), jnp.float32
+    )
+
+    def one(jj, carry):
+        s, part = jj // 2, jj % 2
+        tile, place = jj // per_tile, jj % per_tile
+        pieces = []
+        for ref, count in zip(ins, parts[0]):
+            for b in range(count):
+                lanes = [
+                    ref[:, b, 0, jj * halves + h].reshape(rows, LANES) for h in range(halves)
+                ]
+                tail = ref[:, b, 0, mains + tile].reshape(rows, LANES).astype(jnp.float32)
+                shift = lax.rem(LANES - PIECE * place, LANES)
+                lanes.append(pltpu.roll(tail, shift, axis=1).astype(jnp.bfloat16))
+                pieces.append(jnp.concatenate(lanes, axis=1))
+        fourier = jnp.concatenate(pieces, axis=0)[:, :cols]
+        basis = legendre_ref[s]
+        coeffs = lax.dot_general(
+            fourier, basis, (((0,), (1,)), ((), ())), preferred_element_type=jnp.float32
+        )
+        keep = degree >= wave_ref[step * WAVES_STEP + s]
+        coeffs = jnp.where(keep, coeffs, 0.0)
+        coeff_ref[s, part] = coeffs
+        misfit = jnp.where(keep, coeffs - target_ref[s, part], 0.0)
+        factor = jnp.where(wave_ref[step * WAVES_STEP + s] == 0, 1.0, 2.0)
+        slope = (factor * weight_ref[...]) * misfit
+        loss_ref[...] += jnp.sum(slope * misfit, axis=0, keepdims=True)
+        grad = (2.0 * slope).astype(jnp.bfloat16)
+        flat_ref[:cols, :] = jnp.dot(grad, basis, preferred_element_type=jnp.float32)
+        main = flat_ref[:whole, :].T
+        tail = flat_ref[whole:, :].T
+        offset = 0
+        for ref, count in zip(outs, parts[1]):
+            for b in range(count):
+                for h in range(halves):
+                    value = main[offset : offset + rows, h * LANES : (h + 1) * LANES]
+                    ref[:, b, 0, jj * halves + h] = value.astype(jnp.bfloat16).reshape(
+                        lat, SUB, LANES
+                    )
+                offset += rows
+        grad_tail[tile] += pltpu.roll(tail, PIECE * place, axis=1)
+        return carry
+
+    lax.fori_loop(0, 2 * WAVES_STEP, one, 0)
+    for tile in range(2):
+        offset = 0
+        for ref, count in zip(outs, parts[1]):
+            for b in range(count):
+                value = grad_tail[tile, pl.ds(offset, rows), :]
+                ref[:, b, 0, mains + tile] = value.astype(jnp.bfloat16).reshape(lat, SUB, LANES)
+                offset += rows
+
+
+def middle(lat, first, quarters, splits, waves, weight, legendre, target, arrays):
+    cols, degrees = weight.shape
+    cycles = legendre.shape[2]
+    tiles = arrays[0][0].shape[3]
+    whole = cols // LANES * LANES
+    parts = (tuple(a.shape[1] for a, _ in arrays), tuple(splits))
+
+    def tile_spec(count, start):
+        return pl.BlockSpec(
+            (lat, count, 1, tiles, SUB, LANES), lambda q: (0, 0, q + start, 0, 0, 0)
+        )
+
+    out_specs = [
+        pl.BlockSpec((WAVES_STEP, 2, cols, degrees), lambda q: (q, 0, 0, 0)),
+        pl.BlockSpec((1, degrees), lambda q: (0, 0)),
+    ] + [tile_spec(count, 0) for count in splits]
+    out_shape = [
+        jax.ShapeDtypeStruct((quarters * WAVES_STEP, 2, cols, degrees), jnp.float32),
+        jax.ShapeDtypeStruct((1, degrees), jnp.float32),
+    ] + [
+        jax.ShapeDtypeStruct((lat, count, quarters, tiles, SUB, LANES), jnp.bfloat16)
+        for count in splits
+    ]
+    return pl.pallas_call(
+        functools.partial(middle_kernel, lat, parts),
+        grid=(quarters,),
+        in_specs=[
+            pl.BlockSpec(memory_space=pltpu.SMEM),
+            pl.BlockSpec((cols, degrees), lambda q: (0, 0)),
+            pl.BlockSpec((WAVES_STEP, degrees, cycles), lambda q: (q + first, 0, 0)),
+            pl.BlockSpec((WAVES_STEP, 2, cols, degrees), lambda q: (q + first, 0, 0, 0)),
+        ]
+        + [tile_spec(a.shape[1], start) for a, start in arrays],
+        out_specs=out_specs,
+        out_shape=out_shape,
+        scratch_shapes=[
+            pltpu.VMEM((2, cycles, LANES), jnp.float32),
+            pltpu.VMEM((whole + LANES, cycles), jnp.float32),
+        ],
+        compiler_params=pltpu.CompilerParams(vmem_limit_bytes=60 * 2**20),
+        cost_estimate=pl.CostEstimate(
+            flops=8 * cols * degrees * cycles * WAVES_STEP * quarters,
+            bytes_accessed=20 * cols * degrees * WAVES_STEP * quarters,
+            transcendentals=0,
+        ),
+        name="middle_waves",
+    )(waves, weight, legendre, target, *[a for a, _ in arrays])
+
+
+def backward_kernel(
+    lat, first, groups, len_ref, inv_ref, root_ref, wave_ref, sine_ref, *rest
+):
+    ins = rest[: len(groups)]
+    out_ref, rows_ref, table_ref, main_ref, tail_ref = rest[-5:]
+    cols, _, segment = out_ref.shape
+    width = table_ref.shape[1]
+    whole = cols // LANES * LANES
+    halves = whole // LANES
+    mains = 2 * WAVES_STEP * halves
+    per_tile = WAVES_STEP
+    block = pl.program_id(0) + first
+
+    def collect(owner, carry):
+        quarter = 0
+        for in_ref, quarters in zip(ins, groups):
+            for q in range(quarters):
+                for jj in range(2 * WAVES_STEP):
+                    start = ((quarter * 2 * WAVES_STEP + jj) * lat + owner) * SUB
+                    at = pl.ds(pl.multiple_of(start, SUB), SUB)
+                    for h in range(halves):
+                        value = in_ref[owner, 0, q, jj * halves + h].astype(jnp.float32)
+                        main_ref[h, at, :] = value
+                for t in range(2):
+                    start = ((quarter * 2 + t) * lat + owner) * SUB
+                    at = pl.ds(pl.multiple_of(start, SUB), SUB)
+                    tail_ref[at, :] = in_ref[owner, 0, q, mains + t].astype(jnp.float32)
+                quarter += 1
+        return carry
+
+    lax.fori_loop(0, lat, collect, 0)
+
+    def cycle(r, carry):
+        slot = block * SUB + r
+        make_table(len_ref[slot], inv_ref[slot], root_ref[slot], wave_ref, sine_ref, table_ref)
+        main = [main_ref[h, pl.ds(r, width, stride=SUB), :].T for h in range(halves)]
+        pieces = []
+        for t in range(width // lat // per_tile):
+            value = tail_ref[pl.ds(t * lat * SUB + r, lat, stride=SUB), :]
+            for i in range(per_tile):
+                pieces.append(value if i == 0 else pltpu.roll(value, LANES - PIECE * i, axis=1))
+        tail = jnp.concatenate(pieces, axis=0).T
+        spectrum = jnp.concatenate([*main, tail[: cols - whole]], axis=0).astype(jnp.bfloat16)
+        field = lax.dot_general(
+            spectrum, table_ref[...], (((1,), (1,)), ((), ())), preferred_element_type=jnp.float32
+        )
+        for t in range(segment // LANES):
+            piece = field[:, t * LANES : (t + 1) * LANES]
+            rows_ref[t, pl.ds(r, cols, stride=SUB), :] = piece
+        return carry
+
+    lax.fori_loop(0, SUB, cycle, 0)
+    chunk = 12 if cols % 12 == 0 else 1
+
+    def narrow(i, carry):
+        start = pl.multiple_of(i * chunk * SUB, SUB)
+        for t in range(segment // LANES):
+            value = rows_ref[t, pl.ds(start, chunk * SUB), :].reshape(chunk, SUB, LANES)
+            lanes = slice(t * LANES, (t + 1) * LANES)
+            out_ref[pl.ds(i * chunk, chunk), :, lanes] = value.astype(jnp.bfloat16)
+        return carry
+
+    lax.fori_loop(0, cols // chunk, narrow, 0)
+
+
+def backward(lat, first, blocks, lengths, inverse, root, waves, sine, arrays, shape, done):
+    cols, _, segment = shape
+    width = waves.shape[1]
+    whole = cols // LANES * LANES
+    tiles = arrays[0][0].shape[3]
+    groups = tuple(a.shape[2] for a, _ in arrays)
+    smem = pl.BlockSpec(memory_space=pltpu.SMEM)
+    small = pl.BlockSpec((1, width), lambda b: (0, 0))
+
+    def tile_spec(q, start):
+        return pl.BlockSpec((lat, 1, q, tiles, SUB, LANES), lambda b: (0, b + start, 0, 0, 0, 0))
+
+    extra = [] if done is None else [done]
+    in_specs = [smem, smem, smem, small, small]
+    in_specs += [tile_spec(a.shape[2], start) for a, start in arrays]
+    in_specs += [pl.BlockSpec(memory_space=pl.ANY)] * len(extra)
+    return pl.pallas_call(
+        functools.partial(backward_kernel, lat, first, groups),
+        grid=(blocks,),
+        in_specs=in_specs,
+        out_specs=pl.BlockSpec((cols, SUB, segment), lambda b: (0, b + first, 0)),
+        out_shape=jax.ShapeDtypeStruct(shape, jnp.bfloat16),
+        scratch_shapes=[
+            pltpu.VMEM((segment // LANES, cols * SUB, LANES), jnp.float32),
+            pltpu.VMEM((segment, width), jnp.bfloat16),
+            pltpu.VMEM((whole // LANES, width * SUB, LANES), jnp.float32),
+            pltpu.VMEM((width // WAVES_STEP * SUB, LANES), jnp.float32),
+        ],
+        input_output_aliases={} if done is None else {5 + len(arrays): 0},
+        compiler_params=pltpu.CompilerParams(vmem_limit_bytes=58 * 2**20),
+        cost_estimate=pl.CostEstimate(
+            flops=2 * cols * segment * width * SUB * blocks,
+            bytes_accessed=2 * cols * (segment + width) * SUB * blocks,
+            transcendentals=0,
+        ),
+        name="backward_cycles",
+    )(lengths, inverse, root, waves, sine, *[a for a, _ in arrays], *extra)
+
+
+def exchange(x):
+    return lax.all_to_all(x, "lat", split_axis=0, concat_axis=0, tiled=True)
+
+
+def per_device(lat, grid, cycle_ids, cycle_len, wave_ids, legendre, target, step_w, chan_w):
+    _, batch_size, chan_count, cycle_dev, segment = grid.shape
+    wave_count = wave_ids.shape[0]
+    wave_dev, degrees, cycle_count = legendre.shape
+    cols = batch_size * chan_count
+    lat_index = lax.axis_index("lat")
+    blocks = cycle_dev // SUB
+    quarters = wave_dev // WAVES_STEP
+    early = quarters // 2
+    late = quarters - early
+    rows = grid[0].reshape(cols, cycle_dev, segment)
+
+    my_cycles = lax.dynamic_slice_in_dim(cycle_ids, lat_index * cycle_dev, cycle_dev)
+    lengths = jnp.take(cycle_len, my_cycles)
+    inverse = 1.0 / lengths.astype(jnp.float32)
+    root = lax.rsqrt(lengths.astype(jnp.float32))
+    by_slot = jnp.transpose(wave_ids.reshape(lat, wave_dev))
+    waves = jnp.broadcast_to(by_slot[:, None, :], (wave_dev, 2, lat)).reshape(1, -1)
+    sine = (jnp.arange(2 * wave_dev * lat, dtype=jnp.int32) // lat % 2).reshape(1, -1)
+    tables = (lengths, inverse, root, waves, sine)
+
+    sizes = (1, (blocks - 1) // 2, blocks - 1 - (blocks - 1) // 2)
+    (out0,) = forward(lat, 0, sizes[0], (quarters,), *tables, rows)
+    in0 = exchange(out0)
+    (out1,) = forward(lat, sizes[0], sizes[1], (quarters,), *tables, rows)
+    in1 = exchange(out1)
+    out2, out3 = forward(lat, sizes[0] + sizes[1], sizes[2], (early, late), *tables, rows)
+    in2 = exchange(out2)
+    in3 = exchange(out3)
+
+    order = jnp.transpose(cycle_ids.reshape(lat, blocks, SUB), (1, 0, 2)).reshape(-1)
+    pick = (jnp.arange(cycle_count, dtype=jnp.int32)[:, None] == order[None, :]).astype(jnp.bfloat16)
+    basis = jnp.dot(
+        legendre.reshape(wave_dev * degrees, cycle_count),
+        pick,
+        preferred_element_type=jnp.float32,
+    )
+    basis = basis.astype(jnp.bfloat16).reshape(wave_dev, degrees, cycle_count)
+    my_waves = lax.dynamic_slice_in_dim(wave_ids, lat_index * wave_dev, wave_dev)
+    weight = jnp.broadcast_to(step_w[0] * chan_w[None, :], (batch_size, chan_count))
+    weight = jnp.broadcast_to(weight.reshape(cols, 1), (cols, degrees))
+    goal = jnp.transpose(target[0].reshape(cols, 2, wave_dev, degrees), (2, 1, 0, 3))
+
+    cut = early * WAVES_STEP
+    coeffs_a, loss_a, back0 = middle(
+        lat, 0, early, (blocks,), my_waves[:cut], weight, basis, goal,
+        [(in0, 0), (in1, 0), (in2, 0)],
+    )
+    ret0 = exchange(back0)
+    leave = (sizes[1], sizes[2], sizes[0])
+    coeffs_b, loss_b, back1, back2, back3 = middle(
+        lat, early, late, leave, my_waves[cut:], weight, basis, goal,
+        [(in0, early), (in1, early), (in3, 0)],
+    )
+    ret1 = exchange(back1)
+    ret2 = exchange(back2)
+    ret3 = exchange(back3)
+
+    shape = (cols, cycle_dev, segment)
+    field, start = None, 0
+    for arrived, count in zip((ret1, ret2, ret3), leave):
+        field = backward(lat, start, count, *tables, [(ret0, start), (arrived, 0)], shape, field)
+        start += count
+    field_grad = field.reshape(1, batch_size, chan_count, cycle_dev, segment)
+    coeffs = jnp.concatenate([coeffs_a, coeffs_b], axis=0)
+    coeff_out = jnp.transpose(coeffs, (2, 1, 0, 3)).reshape(
+        1, batch_size, chan_count, 2, wave_dev, degrees
+    )
+    loss_sum = lax.psum(jnp.sum(loss_a + loss_b), ("lat", "fld"))
+    term_count = STEPS * cols * wave_count * (wave_count + 1) // 2
+    loss = loss_sum / jnp.float32(term_count)
+    return (coeff_out, loss, field_grad)
 
 
 def cycle_tables(lengths, waves, is_sine, segment):
@@ -48,7 +490,7 @@
     return table.reshape(lengths.shape[0], segment, waves.shape[0])
 
 
-def per_device(lat, grid, cycle_ids, cycle_len, wave_ids, legendre, target, step_w, chan_w):
+def per_device_simple(lat, grid, cycle_ids, cycle_len, wave_ids, legendre, target, step_w, chan_w):
     _, batch_size, chan_count, cycle_dev, segment = grid.shape
     wave_count = wave_ids.shape[0]
     wave_dev, degrees, cycle_count = legendre.shape
@@ -108,10 +550,33 @@
     return (coeff_out, loss, field_grad)
 
 
+def tiled(lat, grid, legendre):
+    _, batch_size, chan_count, cycle_dev, segment = grid.shape
+    wave_dev, cols = legendre.shape[0], batch_size * chan_count
+    spare = cols % LANES
+    return (
+        cycle_dev % SUB == 0
+        and cycle_dev // SUB >= 3
+        and wave_dev % (2 * WAVES_STEP) == 0
+        and 2 * wave_dev * lat % LANES == 0
+        and legendre.shape[2] % LANES == 0
+        and lat % SUB == 0
+        and segment % RUN == 0
+        and segment % LANES == 0
+        and cols > LANES
+        and 0 < spare <= PIECE
+    )
+
+
+def route(lat, grid, cycle_ids, cycle_len, wave_ids, legendre, *rest):
+    run = per_device if tiled(lat, grid, legendre) else per_device_simple
+    return run(lat, grid, cycle_ids, cycle_len, wave_ids, legendre, *rest)
+
+
 def solution(mesh):
     lat = mesh.shape["lat"]
     return jax.shard_map(
-        lambda *args: per_device(lat, *args),
+        lambda *args: route(lat, *args),
         mesh=mesh,
         in_specs=(
             P("fld", None, None, "lat", None),

time: 1350 us -> 877 us (0.65)
  Pallas kernels: 0 us -> 280 us
  waiting for transfers between devices: 301 us -> 51.5 us
  local copies, waits for them, and re-layouts: 220 us -> 47.6 us
  matrix products: 138 us -> 11.2 us
  other arithmetic: 132 us -> 10.6 us
  starting transfers between devices: 94.9 us -> 34.5 us
    psum x1, blocking collectives: 447 us -> 53.3 us  [per_device(): loss_sum = lax.psum(jnp.sum(loss_a + loss_b), ('lat', 'fld'))]
    all_to_all x0 -> x3, blocking collectives: none -> 384 us  [exchange(): return lax.all_to_all(x, 'lat', split_axis=0, concat_axis=0, tiled=True)]
    pallas_call x0 -> x8, Pallas kernels: none -> 280 us  [the longest x3 109 us: backward(): pl.pallas_call(functools.partial(backward_kernel, lat, first, groups), gr...]
    all_to_all x2 -> x5, waiting for transfers between devices: 301 us -> 51.5 us  [exchange(): return lax.all_to_all(x, 'lat', split_axis=0, concat_axis=0, tiled=True)]
    dot_general x4 -> x1, matrix products: 138 us -> 11.2 us  [per_device(): jnp.dot(legendre.reshape(wave_dev * degrees, cycle_count), pick, preferre...]
    convert_element_type x3 -> x1, local copies, waits for them, and re-layouts: 80.3 us -> 11.9 us  [per_device(): basis = basis.astype(jnp.bfloat16).reshape(wave_dev, degrees, cycle_count)]
    all_to_all x2 -> x5, starting transfers between devices: 94.9 us -> 34.5 us  [exchange(): return lax.all_to_all(x, 'lat', split_axis=0, concat_axis=0, tiled=True)]
    convert_element_type x3 -> x0, other arithmetic: 47.8 us -> none  [the longest x1 47.6 us: cycle_tables(): table = jnp.where(inside, table, 0.0).astype(jnp.bfloat16)]
  transfers between devices with their start and end apart: 2 -> 5, of which waited for: 1 -> 3; matrix products, arithmetic and copies ran while one was open for 9% -> 7% of each run, Pallas kernels for 0% -> 27%
where the time goes in v1:
time: 877 us; the launch traced here: 876 us
  blocking collectives  437 us (50%)
  Pallas kernels  280 us (32%)
  waiting for transfers between devices  51.5 us (6%)
  local copies, waits for them, and re-layouts  47.6 us (5%)
  starting transfers between devices  34.5 us (4%)
  matrix products  11.2 us (1%)
  other arithmetic  10.6 us (1%)
    all_to_all x3, blocking collectives, exchange(): return lax.all_to_all(x, 'lat', split_axis=0, concat_axis=0, tiled=True)  384 us
    pallas_call x3, Pallas kernels, backward(): pl.pallas_call(functools.partial(backward_kernel, lat, first, groups), gr...  109 us
    pallas_call x3, Pallas kernels, forward(): pl.pallas_call(functools.partial(forward_kernel, lat, first, groups), gri...  109 us
    pallas_call x2, Pallas kernels, middle(): pl.pallas_call(functools.partial(middle_kernel, lat, parts), grid=(quarte...  61.2 us
    psum x1, blocking collectives, per_device(): loss_sum = lax.psum(jnp.sum(loss_a + loss_b), ('lat', 'fld'))  53.3 us
    all_to_all x5, waiting for transfers between devices, exchange(): return lax.all_to_all(x, 'lat', split_axis=0, concat_axis=0, tiled=True)  51.5 us
    all_to_all x5, starting transfers between devices, exchange(): return lax.all_to_all(x, 'lat', split_axis=0, concat_axis=0, tiled=True)  34.5 us
    transpose x1, local copies, waits for them, and re-layouts, per_device(): jnp.transpose(coeffs, (2, 1, 0, 3))  17.9 us
  transfers between devices with their start and end apart: 5, of which 3 were waited for; matrix products, arithmetic and copies ran while one was open for 7% of the time, Pallas kernels for 27%

profile of v1, /device:TPU:0, one launch (start us, length us, event | category | flops | bytes accessed | tf_op | source)
XLA Modules:
  0.0 875.6 jit_solution(9368996163424603062)
XLA Ops:
  6.2 23.6 %forward_cycles.3 = bf16[16,1,4,22,8,128]{5,4,3,2,1,0:T(8,128)(2,1)} custom-call(s32[40]{0:T(128)} %copy-done.5, f32[40]{0:T(128)} %convert_divide_fusion.inv_ref, f32[40]{0:T(128)} %get-tuple-element.26.root_ref, s32[1,640]{1,0:T(1,128)} %reshape.110.wave_ref, s32[1,640]{1,0:T(1,128)} %and_select_fusion.sine_ref, bf16[276,40,1408]{2,1,0:T(8,128)(2,1)} %bitcast.19), custom_call_target="tpu_custom_call" | custom-call | flops 3979345920 | bytes 9043968 | tf_op jit(solution)/shard_map/forward_cycles/pallas_call | solution.py:139
  29.8 8.3 all-to-all-start
  38.1 42.8 %forward_cycles.5 = (bf16[16,2,2,22,8,128]{5,4,3,2,1,0:T(8,128)(2,1)}, bf16[16,2,2,22,8,128]{5,4,3,2,1,0:T(8,128)(2,1)}) custom-call(s32[40]{0:T(128)} %copy-done.5, f32[40]{0:T(128)} %convert_divide_fusion.inv_ref, f32[40]{0:T(128)} %get-tuple-element.26.root_ref, s32[1,640]{1,0:T(1,128)} %reshape.110.wave_ref, s32[1,640]{1,0:T(1,128)} %and_select_fusion.sine_ref, ...), custom_call_target="tpu_custom_call" | custom-call | flops 7958691840 | bytes 18087936 | tf_op jit(solution)/shard_map/forward_cycles/pallas_call | solution.py:139
  81.0 13.5 %all-to-all-done.rest_0_ = bf16[16,1,4,22,8,128]{5,4,3,2,1,0:T(8,128)(2,1)S(1)} async-done(((bf16[16,1,4,22,8,128]{5,4,3,2,1,0:T(8,128)(2,1)}), bf16[16,1,4,22,8,128]{5,4,3,2,1,0:T(8,128)(2,1)S(1)}, u32[]{:S(2)}, u32[]{:S(2)}) %all-to-all-start) | async-done | bytes 2883616 | tf_op jit(solution)/shard_map/all_to_all | solution.py:396
  94.5 13.9 %all-to-all-start.3 = ((bf16[16,2,2,22,8,128]{5,4,3,2,1,0:T(8,128)(2,1)}), bf16[16,2,2,22,8,128]{5,4,3,2,1,0:T(8,128)(2,1)}, u32[]{:S(2)}, u32[]{:S(2)}) async-start(bf16[16,2,2,22,8,128]{5,4,3,2,1,0:T(8,128)(2,1)} %get-tuple-element.15), calls=%async_computation.3 | async-start | bytes 5767168 | tf_op jit(solution)/shard_map/all_to_all | solution.py:396
  108.4 42.9 %forward_cycles.4 = bf16[16,2,4,22,8,128]{5,4,3,2,1,0:T(8,128)(2,1)} custom-call(s32[40]{0:T(128)} %copy-done.5, f32[40]{0:T(128)} %convert_divide_fusion.inv_ref, f32[40]{0:T(128)} %get-tuple-element.26.root_ref, s32[1,640]{1,0:T(1,128)} %reshape.110.wave_ref, s32[1,640]{1,0:T(1,128)} %and_select_fusion.sine_ref, bf16[276,40,1408]{2,1,0:T(8,128)(2,1)} %bitcast.21), custom_call_target="tpu_custom_call" | custom-call | flops 7958691840 | bytes 18087936 | tf_op jit(solution)/shard_map/forward_cycles/pallas_call | solution.py:139
  151.3 13.2 %all-to-all-done.3.rest_2_ = bf16[16,2,2,22,8,128]{5,4,3,2,1,0:T(8,128)(2,1)} async-done(((bf16[16,2,2,22,8,128]{5,4,3,2,1,0:T(8,128)(2,1)}), bf16[16,2,2,22,8,128]{5,4,3,2,1,0:T(8,128)(2,1)}, u32[]{:S(2)}, u32[]{:S(2)}) %all-to-all-start.3) | async-done | bytes 2883616 | tf_op jit(solution)/shard_map/all_to_all | solution.py:396
  164.5 140.2 %all_to_all.40.rest_1_ = bf16[16,2,4,22,8,128]{5,4,3,2,1,0:T(8,128)(2,1)} all-to-all(bf16[16,2,4,22,8,128]{5,4,3,2,1,0:T(8,128)(2,1)} %forward_cycles.4), channel_id=1, replica_groups=mesh['lat'=16,'fld'=2] {'lat'}, dimensions={0} | all-to-all | bytes 11534336 | tf_op jit(solution)/shard_map/all_to_all | solution.py:396
  304.7 4.1 all-to-all-start.2
  310.6 11.2 %fusion = bf16[6400,640]{0,1:T(8,128)(2,1)} fusion(bf16[6400,640]{1,0:T(8,128)(2,1)} %bitcast.30, s32[640]{0:T(1024)S(1)} %eq.18), kind=kOutput, calls=%fused_computation.4 | convolution fusion | flops 5247795200 | bytes 16386560 | tf_op jit(solution)/shard_map/dot_general | solution.py:431
  321.7 11.9 %copy.17 = bf16[6400,640]{1,0:T(8,128)(2,1)} copy(bf16[6400,640]{0,1:T(8,128)(2,1)} %fusion) | data formatting | bytes 16384000 | tf_op jit(solution)/shard_map/convert_element_type | solution.py:436
  333.6 13.2 %copy.22 = f32[276,2,20,320]{3,0,1,2:T(8,128)} copy(f32[276,2,20,320]{3,1,2,0:T(2,128)} %bitcast.26) | data formatting | bytes 28262400 | tf_op jit(solution)/shard_map/reshape;squeeze | solution.py:440
  348.2 30.6 %middle_waves.3 = (f32[10,2,276,320]{3,2,1,0:T(8,128)}, f32[1,320]{1,0:T(1,128)}, bf16[16,2,2,22,8,128]{5,4,3,2,1,0:T(8,128)(2,1)}, bf16[16,2,2,22,8,128]{5,4,3,...) custom-call(s32[10]{0:T(128)} %get-tuple-element.29.wave_ref, f32[276,320]{1,0:T(8,128)} %broadcast_in_dim.30.weight_ref, ...), custom_call_target="tpu_custom_call" | custom-call | flops 4521984000 | bytes 17664000 | tf_op jit(solution)/shard_map/middle_waves/pallas_call | solution.py:265
  378.8 71.9 %all_to_all.41.rest_1_ = bf16[16,2,2,22,8,128]{5,4,3,2,1,0:T(8,128)(2,1)} all-to-all(bf16[16,2,2,22,8,128]{5,4,3,2,1,0:T(8,128)(2,1)} %get-tuple-element.21), channel_id=1, replica_groups=mesh['lat'=16,'fld'=2] {'lat'}, dimensions={0} | all-to-all | bytes 5767168 | tf_op jit(solution)/shard_map/all_to_all | solution.py:396
  454.5 30.6 %middle_waves.2 = (f32[10,2,276,320]{3,2,1,0:T(8,128)}, f32[1,320]{1,0:T(1,128)}, bf16[16,5,2,22,8,128]{5,4,3,2,1,0:T(8,128)(2,1)}) custom-call(s32[10]{0:T(128)} %get-tuple-element.28.wave_ref, f32[276,320]{1,0:T(8,128)} %broadcast_in_dim.30.weight_ref, bf16[20,320,640]{2,1,0:T(8,128)(2,1)} %bitcast.25, f32[20,2,276,320]{3,2,1,0:T(8,128)} %bitcast.23, ...), custom_call_target="tpu_custom_call" | custom-call | flops 4521984000 | bytes 17664000 | tf_op jit(solution)/shard_map/middle_waves/pallas_call | solution.py:265
  485.1 24.8 %all-to-all-done.7.rest_1_ = bf16[16,2,2,22,8,128]{5,4,3,2,1,0:T(8,128)(2,1)S(1)} async-done(((bf16[16,2,2,22,8,128]{5,4,3,2,1,0:T(8,128)(2,1)}), bf16[16,2,2,22,8,128]{5,4,3,2,1,0:T(8,128)(2,1)S(1)}, u32[]{:S(2)}, u32[]{:S(2)}) %all-to-all-start.7) | async-done | bytes 2883616 | tf_op jit(solution)/shard_map/all_to_all | solution.py:396
  509.9 171.5 %all_to_all.42.rest_0_ = bf16[16,5,2,22,8,128]{5,4,3,2,1,0:T(8,128)(2,1)} all-to-all(bf16[16,5,2,22,8,128]{5,4,3,2,1,0:T(8,128)(2,1)} %get-tuple-element.19), channel_id=1, replica_groups=mesh['lat'=16,'fld'=2] {'lat'}, dimensions={0} | all-to-all | bytes 14417920 | tf_op jit(solution)/shard_map/all_to_all | solution.py:396
  681.4 4.4 all-to-all-start.5
  686.5 53.3 %psum.7 = f32[]{:T(128)} all-reduce(f32[]{:T(128)} %add_reduce_fusion), channel_id=1, replica_groups=mesh['lat'=16,'fld'=2] {'lat','fld'}, use_global_device_ids=true, to_apply=%region_1.2 | all-reduce | flops 1 | bytes 8 | tf_op jit(solution)/shard_map/psum | solution.py:467
  739.8 6.7 maximum_bitcast_fusion
  746.5 17.9 %copy.20 = f32[276,2,20,320]{3,1,2,0:T(2,128)} copy(f32[276,2,20,320]{3,0,1,2:T(8,128)S(1)} %maximum_bitcast_fusion) | data formatting | bytes 28262400 | tf_op jit(solution)/shard_map/transpose | solution.py:464
  765.0 42.9 %backward_cycles.3.rest_2_ = bf16[276,40,1408]{2,1,0:T(8,128)(2,1)} custom-call(s32[40]{0:T(128)} %copy-done.5, f32[40]{0:T(128)} %convert_divide_fusion.inv_ref, f32[40]{0:T(128)} %get-tuple-element.26.root_ref, s32[1,640]{1,0:T(1,128)} %reshape.110.wave_ref, s32[1,640]{1,0:T(1,128)} %and_select_fusion.sine_ref, ...), custom_call_target="tpu_custom_call" | custom-call | flops 7958691840 | bytes 18087936 | tf_op jit(solution)/shard_map/backward_cycles/pallas_call | solution.py:372
  807.9 42.9 %backward_cycles.4.rest_2_ = bf16[276,40,1408]{2,1,0:T(8,128)(2,1)} custom-call(s32[40]{0:T(128)} %copy-done.5, f32[40]{0:T(128)} %convert_divide_fusion.inv_ref, f32[40]{0:T(128)} %get-tuple-element.26.root_ref, s32[1,640]{1,0:T(1,128)} %reshape.110.wave_ref, s32[1,640]{1,0:T(1,128)} %and_select_fusion.sine_ref, ...), custom_call_target="tpu_custom_call", output_to_operand_aliasing={{}: (7, {})} | custom-call | flops 7958691840 | bytes 18087936 | tf_op jit(solution)/shard_map/backward_cycles/pallas_call | solution.py:372
  850.8 23.6 %backward_cycles.5 = bf16[276,40,1408]{2,1,0:T(8,128)(2,1)} custom-call(s32[40]{0:T(128)} %copy-done.5, f32[40]{0:T(128)} %convert_divide_fusion.inv_ref, f32[40]{0:T(128)} %get-tuple-element.26.root_ref, s32[1,640]{1,0:T(1,128)} %reshape.110.wave_ref, s32[1,640]{1,0:T(1,128)} %and_select_fusion.sine_ref, ...), custom_call_target="tpu_custom_call", output_to_operand_aliasing={{}: (7, {})} | custom-call | flops 3979345920 | bytes 9043968 | tf_op jit(solution)/shard_map/backward_cycles/pallas_call | solution.py:372
  (43 shorter events, 12.4 us)
Async XLA Ops:
  0.6 1.4 copy-start
  4.1 2.1 copy-start.5
  29.8 64.7 %all-to-all-start = ((bf16[16,1,4,22,8,128]{5,4,3,2,1,0:T(8,128)(2,1)}), bf16[16,1,4,22,8,128]{5,4,3,2,1,0:T(8,128)(2,1)S(1)}, u32[]{:S(2)}, u32[]{:S(2)}) async-start(bf16[16,1,4,22,8,128]{5,4,3,2,1,0:T(8,128)(2,1)} %forward_cycles.3), calls=%async_computation | async-start | bytes 5767168 | tf_op jit(solution)/shard_map/all_to_all | solution.py:396
  94.5 56.8 %copy-start.2 = (bf16[16,1,4,22,8,128]{5,4,3,2,1,0:T(8,128)(2,1)}, bf16[16,1,4,22,8,128]{5,4,3,2,1,0:T(8,128)(2,1)S(1)}, u32[]{:S(2)}) copy-start(bf16[16,1,4,22,8,128]{5,4,3,2,1,0:T(8,128)(2,1)S(1)} %all-to-all-done.rest_0_) | copy-start | bytes 8650756
  94.5 70.0 %all-to-all-start.3 = ((bf16[16,2,2,22,8,128]{5,4,3,2,1,0:T(8,128)(2,1)}), bf16[16,2,2,22,8,128]{5,4,3,2,1,0:T(8,128)(2,1)}, u32[]{:S(2)}, u32[]{:S(2)}) async-start(bf16[16,2,2,22,8,128]{5,4,3,2,1,0:T(8,128)(2,1)} %get-tuple-element.15), calls=%async_computation.3 | async-start | bytes 5767168 | tf_op jit(solution)/shard_map/all_to_all | solution.py:396
  151.3 157.6 %copy-start.6 = (s32[640]{0:T(1024)S(1)}, s32[640]{0:T(1024)}, u32[]{:S(2)}) copy-start(s32[640]{0:T(1024)} %param.9) | copy-start | bytes 7684
  151.3 159.1 %copy-start.9 = (f32[69]{0:T(128)S(1)}, f32[69]{0:T(128)}, u32[]{:S(2)}) copy-start(f32[69]{0:T(128)} %param.15) | copy-start | bytes 832
  304.7 74.1 %all-to-all-start.2 = ((bf16[16,2,2,22,8,128]{5,4,3,2,1,0:T(8,128)(2,1)}), bf16[16,2,2,22,8,128]{5,4,3,2,1,0:T(8,128)(2,1)S(1)}, u32[]{:S(2)}, u32[]{:S(2)}) async-start(bf16[16,2,2,22,8,128]{5,4,3,2,1,0:T(8,128)(2,1)} %get-tuple-element.13), calls=%async_computation.2 | async-start | bytes 5767168 | tf_op jit(solution)/shard_map/all_to_all | solution.py:396
  378.8 71.9 %copy-start.4 = (bf16[16,2,2,22,8,128]{5,4,3,2,1,0:T(8,128)(2,1)}, bf16[16,2,2,22,8,128]{5,4,3,2,1,0:T(8,128)(2,1)S(1)}, u32[]{:S(2)}) copy-start(bf16[16,2,2,22,8,128]{5,4,3,2,1,0:T(8,128)(2,1)S(1)} %all-to-all-done.2.rest_2_) | copy-start | bytes 8650756
  450.8 59.1 %all-to-all-start.7 = ((bf16[16,2,2,22,8,128]{5,4,3,2,1,0:T(8,128)(2,1)}), bf16[16,2,2,22,8,128]{5,4,3,2,1,0:T(8,128)(2,1)S(1)}, u32[]{:S(2)}, u32[]{:S(2)}) async-start(bf16[16,2,2,22,8,128]{5,4,3,2,1,0:T(8,128)(2,1)} %get-tuple-element.22), calls=%async_computation.7 | async-start | bytes 5767168 | tf_op jit(solution)/shard_map/all_to_all | solution.py:396
  509.9 171.5 %copy-start.3 = (bf16[16,2,2,22,8,128]{5,4,3,2,1,0:T(8,128)(2,1)}, bf16[16,2,2,22,8,128]{5,4,3,2,1,0:T(8,128)(2,1)S(1)}, u32[]{:S(2)}) copy-start(bf16[16,2,2,22,8,128]{5,4,3,2,1,0:T(8,128)(2,1)S(1)} %all-to-all-done.7.rest_1_) | copy-start | bytes 8650756
  509.9 175.9 %copy-start.7 = (f32[1,320]{1,0:T(1,128)S(1)}, f32[1,320]{1,0:T(1,128)}, u32[]{:S(2)}) copy-start(f32[1,320]{1,0:T(1,128)} %get-tuple-element.18) | copy-start | bytes 3844
  509.9 175.9 %copy-start.8 = (f32[1,320]{1,0:T(1,128)S(1)}, f32[1,320]{1,0:T(1,128)}, u32[]{:S(2)}) copy-start(f32[1,320]{1,0:T(1,128)} %get-tuple-element.17) | copy-start | bytes 3844
  681.4 169.4 %all-to-all-start.5 = ((bf16[16,1,2,22,8,128]{5,4,3,2,1,0:T(8,128)(2,1)}), bf16[16,1,2,22,8,128]{5,4,3,2,1,0:T(8,128)(2,1)}, u32[]{:S(2)}, u32[]{:S(2)}) async-start(bf16[16,1,2,22,8,128]{5,4,3,2,1,0:T(8,128)(2,1)} %get-tuple-element.20), calls=%async_computation.5 | async-start | bytes 2883584 | tf_op jit(solution)/shard_map/all_to_all | solution.py:396
  850.8 23.7 %copy-start.1 = (s32[640]{0:T(1024)S(1)}, s32[640]{0:T(1024)}, u32[]{:S(2)}) copy-start(s32[640]{0:T(1024)} %param.10) | copy-start | bytes 7684

commit v2 on v1

--- a/solution.py
+++ b/solution.py
@@ -12,8 +12,10 @@
 STEPS = 2
 LANES = 128
 SUB = 8
-RUN = 64
+RUN = 32
 WAVES_STEP = 5
+TERMS = 3
+SPARE = 120
 PIECE = 24
 
 
@@ -41,8 +43,8 @@
 def make_table(length, inverse, root, wave_ref, sine_ref, table_ref):
     segment, width = table_ref.shape
 
-    def lane_tile(tile, carry):
-        lanes = pl.ds(pl.multiple_of(tile * LANES, LANES), LANES)
+    for tile in range(width // LANES):
+        lanes = slice(tile * LANES, (tile + 1) * LANES)
         wave = wave_ref[:, lanes]
         is_sine = sine_ref[:, lanes] == 1
         row = lax.broadcasted_iota(jnp.int32, (RUN, LANES), 0)
@@ -54,20 +56,16 @@
         now = before * cos_run + slope * sin_run
         twice = 2.0 * cos_run
         for step in range(segment // RUN):
-            value = jnp.where(row < length - step * RUN, before, 0.0)
-            table_ref[pl.ds(step * RUN, RUN), lanes] = value.astype(jnp.bfloat16)
+            table_ref[pl.ds(step * RUN, RUN), lanes] = before.astype(jnp.bfloat16)
             before, now = now, twice * now - before
-        return carry
-
-    lax.fori_loop(0, width // LANES, lane_tile, 0)
 
 
 def forward_kernel(
     lat, first, groups, len_ref, inv_ref, root_ref, wave_ref, sine_ref, grid_ref, *rest
 ):
-    outs, (rows_ref, table_ref, flat_ref, main_ref, tail_ref) = rest[:-5], rest[-5:]
+    outs, (rows_ref, even_ref, odd_ref, flat_ref, main_ref, tail_ref) = rest[:-6], rest[-6:]
     cols, _, segment = grid_ref.shape
-    width = table_ref.shape[1]
+    width = even_ref.shape[1]
     whole = cols // LANES * LANES
     per_tile = 2 * WAVES_STEP // 2
     block = pl.program_id(0) + first
@@ -85,13 +83,19 @@
     pad = flat_ref.shape[0]
     flat_ref[cols // SUB * SUB :, :] = jnp.zeros((pad - cols // SUB * SUB, width), jnp.float32)
 
-    def cycle(r, carry):
-        slot = block * SUB + r
+    last = (first + pl.num_programs(0)) * SUB - 1
+
+    def prepare(r, table_ref):
+        slot = jnp.minimum(block * SUB + r, last)
         make_table(len_ref[slot], inv_ref[slot], root_ref[slot], wave_ref, sine_ref, table_ref)
-        rows = [
-            rows_ref[t, pl.ds(r, cols, stride=SUB), :].astype(jnp.bfloat16)
-            for t in range(segment // LANES)
-        ]
+
+    def cycle(r, table_ref):
+        length = len_ref[block * SUB + r]
+        lane = lax.broadcasted_iota(jnp.int32, (cols, LANES), 1)
+        rows = []
+        for t in range(segment // LANES):
+            piece = rows_ref[t, pl.ds(r, cols, stride=SUB), :]
+            rows.append(jnp.where(lane < length - t * LANES, piece, 0.0).astype(jnp.bfloat16))
         rows = jnp.concatenate(rows, axis=1)
         flat_ref[:cols, :] = jnp.dot(rows, table_ref[...], preferred_element_type=jnp.float32)
         for h in range(whole // LANES):
@@ -103,9 +107,19 @@
             for i in range(1, per_tile):
                 total = total + pltpu.roll(tail[t * per_tile + i], PIECE * i, axis=1)
             tail_ref[pl.ds(t * lat * SUB + r, lat, stride=SUB), :] = total
+
+    def two(i, carry):
+        prepare(2 * i + 1, odd_ref)
+        cycle(2 * i, even_ref)
+        prepare(2 * i + 2, even_ref)
+        cycle(2 * i + 1, odd_ref)
         return carry
 
-    lax.fori_loop(0, SUB, cycle, 0)
+    @pl.when(pl.program_id(0) == 0)
+    def _():
+        prepare(0, even_ref)
+
+    lax.fori_loop(0, SUB // 2, two, 0)
 
     halves = whole // LANES
     mains = 2 * WAVES_STEP * halves
@@ -150,6 +164,7 @@
         scratch_shapes=[
             pltpu.VMEM((segment // LANES, cols * SUB, LANES), jnp.float32),
             pltpu.VMEM((segment, width), jnp.bfloat16),
+            pltpu.VMEM((segment, width), jnp.bfloat16),
             pltpu.VMEM((whole + LANES, width), jnp.float32),
             pltpu.VMEM((whole // LANES, width * SUB, LANES), jnp.float32),
             pltpu.VMEM((width // WAVES_STEP * SUB, LANES), jnp.float32),
@@ -164,7 +179,7 @@
     )(lengths, inverse, root, waves, sine, rows)
 
 
-def middle_kernel(lat, parts, wave_ref, weight_ref, legendre_ref, target_ref, *rest):
+def middle_kernel(lat, parts, wave_ref, weight_ref, before_ref, legendre_ref, target_ref, *rest):
     ins = rest[: len(parts[0])]
     rest = rest[len(parts[0]) :]
     coeff_ref, loss_ref = rest[:2]
@@ -181,7 +196,7 @@
 
     @pl.when(step == 0)
     def _():
-        loss_ref[...] = jnp.zeros_like(loss_ref)
+        loss_ref[...] = before_ref[...]
 
     grad_tail[...] = jnp.zeros_like(grad_tail)
     flat_ref[cols // SUB * SUB :, :] = jnp.zeros(
@@ -230,16 +245,25 @@
         return carry
 
     lax.fori_loop(0, 2 * WAVES_STEP, one, 0)
+    lane = lax.broadcasted_iota(jnp.int32, (rows, LANES), 1)
+    left = jnp.sum(loss_ref[...], axis=1, keepdims=True)
+    total = jnp.zeros((rows, LANES), jnp.float32)
+    for n in range(TERMS):
+        term = left.astype(jnp.bfloat16).astype(jnp.float32)
+        left = left - term
+        total = jnp.where(lane == SPARE + n, term, total)
     for tile in range(2):
         offset = 0
         for ref, count in zip(outs, parts[1]):
             for b in range(count):
                 value = grad_tail[tile, pl.ds(offset, rows), :]
+                if tile == 0 and offset == 0:
+                    value = value + total
                 ref[:, b, 0, mains + tile] = value.astype(jnp.bfloat16).reshape(lat, SUB, LANES)
                 offset += rows
 
 
-def middle(lat, first, quarters, splits, waves, weight, legendre, target, arrays):
+def middle(lat, first, quarters, splits, waves, weight, before, legendre, target, arrays):
     cols, degrees = weight.shape
     cycles = legendre.shape[2]
     tiles = arrays[0][0].shape[3]
@@ -268,6 +292,7 @@
         in_specs=[
             pl.BlockSpec(memory_space=pltpu.SMEM),
             pl.BlockSpec((cols, degrees), lambda q: (0, 0)),
+            pl.BlockSpec((1, degrees), lambda q: (0, 0)),
             pl.BlockSpec((WAVES_STEP, degrees, cycles), lambda q: (q + first, 0, 0)),
             pl.BlockSpec((WAVES_STEP, 2, cols, degrees), lambda q: (q + first, 0, 0, 0)),
         ]
@@ -285,16 +310,16 @@
             transcendentals=0,
         ),
         name="middle_waves",
-    )(waves, weight, legendre, target, *[a for a, _ in arrays])
+    )(waves, weight, before, legendre, target, *[a for a, _ in arrays])
 
 
 def backward_kernel(
     lat, first, groups, len_ref, inv_ref, root_ref, wave_ref, sine_ref, *rest
 ):
     ins = rest[: len(groups)]
-    out_ref, rows_ref, table_ref, main_ref, tail_ref = rest[-5:]
+    out_ref, rows_ref, even_ref, odd_ref, main_ref, tail_ref = rest[-6:]
     cols, _, segment = out_ref.shape
-    width = table_ref.shape[1]
+    width = even_ref.shape[1]
     whole = cols // LANES * LANES
     halves = whole // LANES
     mains = 2 * WAVES_STEP * halves
@@ -320,9 +345,13 @@
 
     lax.fori_loop(0, lat, collect, 0)
 
-    def cycle(r, carry):
-        slot = block * SUB + r
+    last = (first + pl.num_programs(0)) * SUB - 1
+
+    def prepare(r, table_ref):
+        slot = jnp.minimum(block * SUB + r, last)
         make_table(len_ref[slot], inv_ref[slot], root_ref[slot], wave_ref, sine_ref, table_ref)
+
+    def cycle(r, table_ref):
         main = [main_ref[h, pl.ds(r, width, stride=SUB), :].T for h in range(halves)]
         pieces = []
         for t in range(width // lat // per_tile):
@@ -334,12 +363,25 @@
         field = lax.dot_general(
             spectrum, table_ref[...], (((1,), (1,)), ((), ())), preferred_element_type=jnp.float32
         )
+        length = len_ref[block * SUB + r]
+        lane = lax.broadcasted_iota(jnp.int32, (cols, LANES), 1)
         for t in range(segment // LANES):
             piece = field[:, t * LANES : (t + 1) * LANES]
+            piece = jnp.where(lane < length - t * LANES, piece, 0.0)
             rows_ref[t, pl.ds(r, cols, stride=SUB), :] = piece
+
+    def two(i, carry):
+        prepare(2 * i + 1, odd_ref)
+        cycle(2 * i, even_ref)
+        prepare(2 * i + 2, even_ref)
+        cycle(2 * i + 1, odd_ref)
         return carry
 
-    lax.fori_loop(0, SUB, cycle, 0)
+    @pl.when(pl.program_id(0) == 0)
+    def _():
+        prepare(0, even_ref)
+
+    lax.fori_loop(0, SUB // 2, two, 0)
     chunk = 12 if cols % 12 == 0 else 1
 
     def narrow(i, carry):
@@ -378,6 +420,7 @@
         scratch_shapes=[
             pltpu.VMEM((segment // LANES, cols * SUB, LANES), jnp.float32),
             pltpu.VMEM((segment, width), jnp.bfloat16),
+            pltpu.VMEM((segment, width), jnp.bfloat16),
             pltpu.VMEM((whole // LANES, width * SUB, LANES), jnp.float32),
             pltpu.VMEM((width // WAVES_STEP * SUB, LANES), jnp.float32),
         ],
@@ -417,14 +460,11 @@
     sine = (jnp.arange(2 * wave_dev * lat, dtype=jnp.int32) // lat % 2).reshape(1, -1)
     tables = (lengths, inverse, root, waves, sine)
 
-    sizes = (1, (blocks - 1) // 2, blocks - 1 - (blocks - 1) // 2)
-    (out0,) = forward(lat, 0, sizes[0], (quarters,), *tables, rows)
+    (out0,) = forward(lat, 0, 1, (quarters,), *tables, rows)
     in0 = exchange(out0)
-    (out1,) = forward(lat, sizes[0], sizes[1], (quarters,), *tables, rows)
+    out1, out2 = forward(lat, 1, blocks - 1, (early, late), *tables, rows)
     in1 = exchange(out1)
-    out2, out3 = forward(lat, sizes[0] + sizes[1], sizes[2], (early, late), *tables, rows)
     in2 = exchange(out2)
-    in3 = exchange(out3)
 
     order = jnp.transpose(cycle_ids.reshape(lat, blocks, SUB), (1, 0, 2)).reshape(-1)
     pick = (jnp.arange(cycle_count, dtype=jnp.int32)[:, None] == order[None, :]).astype(jnp.bfloat16)
@@ -440,15 +480,16 @@
     goal = jnp.transpose(target[0].reshape(cols, 2, wave_dev, degrees), (2, 1, 0, 3))
 
     cut = early * WAVES_STEP
+    nothing = jnp.zeros((1, degrees), jnp.float32)
     coeffs_a, loss_a, back0 = middle(
-        lat, 0, early, (blocks,), my_waves[:cut], weight, basis, goal,
-        [(in0, 0), (in1, 0), (in2, 0)],
+        lat, 0, early, (blocks,), my_waves[:cut], weight, nothing, basis, goal,
+        [(in0, 0), (in1, 0)],
     )
     ret0 = exchange(back0)
-    leave = (sizes[1], sizes[2], sizes[0])
-    coeffs_b, loss_b, back1, back2, back3 = middle(
-        lat, early, late, leave, my_waves[cut:], weight, basis, goal,
-        [(in0, early), (in1, early), (in3, 0)],
+    leave = ((blocks - 1) // 2, blocks - 1 - (blocks - 1) // 2, 1)
+    coeffs_b, _, back1, back2, back3 = middle(
+        lat, early, late, leave, my_waves[cut:], weight, loss_a, basis, goal,
+        [(in0, early), (in2, 0)],
     )
     ret1 = exchange(back1)
     ret2 = exchange(back2)
@@ -464,7 +505,11 @@
     coeff_out = jnp.transpose(coeffs, (2, 1, 0, 3)).reshape(
         1, batch_size, chan_count, 2, wave_dev, degrees
     )
-    loss_sum = lax.psum(jnp.sum(loss_a + loss_b), ("lat", "fld"))
+    pieces = ret1[:, 0, late - 1, -2, 0, SPARE : SPARE + TERMS]
+    loss_sum = jnp.sum(jnp.sum(pieces.astype(jnp.float32), axis=1))
+    loss_sum = jnp.broadcast_to(loss_sum, (SUB, LANES))
+    other = lax.ppermute(loss_sum, "fld", [(0, 1), (1, 0)])
+    loss_sum = loss_sum[0, 0] + other[0, 0]
     term_count = STEPS * cols * wave_count * (wave_count + 1) // 2
     loss = loss_sum / jnp.float32(term_count)
     return (coeff_out, loss, field_grad)
@@ -565,6 +610,8 @@
         and segment % LANES == 0
         and cols > LANES
         and 0 < spare <= PIECE
+        and PIECE * WAVES_STEP <= SPARE
+        and lax.axis_size("fld") == 2
     )
 
 

time: 877 us -> 809 us (0.922)
  Pallas kernels: 280 us -> 215 us
  blocking collectives: 437 us -> 464 us
  starting transfers between devices: 34.5 us -> 18 us
  waiting for transfers between devices: 51.5 us -> 36.1 us
    all_to_all x3 -> x4, blocking collectives: 384 us -> 464 us  [exchange(): return lax.all_to_all(x, 'lat', split_axis=0, concat_axis=0, tiled=True)]
    psum x1 -> x0, blocking collectives: 53.3 us -> none  [per_device(): loss_sum = lax.psum(jnp.sum(loss_a + loss_b), ('lat', 'fld'))]
    pallas_call x3 -> x2, Pallas kernels: 109 us -> 72.6 us  [forward(): pl.pallas_call(functools.partial(forward_kernel, lat, first, groups), gri...]
    pallas_call x3, Pallas kernels: 109 us -> 81 us  [backward(): pl.pallas_call(functools.partial(backward_kernel, lat, first, groups), gr...]
    all_to_all x5 -> x3, starting transfers between devices: 34.5 us -> 17.9 us  [exchange(): return lax.all_to_all(x, 'lat', split_axis=0, concat_axis=0, tiled=True)]
    all_to_all x5 -> x3, waiting for transfers between devices: 51.5 us -> 36.1 us  [exchange(): return lax.all_to_all(x, 'lat', split_axis=0, concat_axis=0, tiled=True)]
  transfers between devices with their start and end apart: 5 -> 4, of which waited for: 3 -> 2; matrix products, arithmetic and copies ran while one was open for 7% -> 8% of each run, Pallas kernels for 27% -> 18%
where the time goes in v2:
time: 809 us; the launch traced here: 808 us
  blocking collectives  464 us (57%)
  Pallas kernels  215 us (27%)
  local copies, waits for them, and re-layouts  49.5 us (6%)
  waiting for transfers between devices  36.1 us (4%)
  starting transfers between devices  18 us (2%)
  matrix products  11.2 us (1%)
  other arithmetic  10.7 us (1%)
    all_to_all x4, blocking collectives, exchange(): return lax.all_to_all(x, 'lat', split_axis=0, concat_axis=0, tiled=True)  464 us
    pallas_call x3, Pallas kernels, backward(): pl.pallas_call(functools.partial(backward_kernel, lat, first, groups), gr...  81 us
    pallas_call x2, Pallas kernels, forward(): pl.pallas_call(functools.partial(forward_kernel, lat, first, groups), gri...  72.6 us
    pallas_call x2, Pallas kernels, middle(): pl.pallas_call(functools.partial(middle_kernel, lat, parts), grid=(quarte...  61.3 us
    all_to_all x3, waiting for transfers between devices, exchange(): return lax.all_to_all(x, 'lat', split_axis=0, concat_axis=0, tiled=True)  36.1 us
    all_to_all x3, starting transfers between devices, exchange(): return lax.all_to_all(x, 'lat', split_axis=0, concat_axis=0, tiled=True)  17.9 us
    transpose x1, local copies, waits for them, and re-layouts, per_device(): jnp.transpose(coeffs, (2, 1, 0, 3))  17.9 us
  transfers between devices with their start and end apart: 4, of which 2 were waited for; matrix products, arithmetic and copies ran while one was open for 8% of the time, Pallas kernels for 18%

profile of v2, /device:TPU:0, one launch (start us, length us, event | category | flops | bytes accessed | tf_op | source)
XLA Modules:
  0.0 807.6 jit_solution(15615358728875605743)
XLA Ops:
  2.8 1.3 convert_rsqrt_fusion
  4.6 0.8 reshape.110
  6.2 17.5 %forward_cycles.2 = bf16[16,1,4,22,8,128]{5,4,3,2,1,0:T(8,128)(2,1)} custom-call(s32[40]{0:T(128)} %copy-done.4, f32[40]{0:T(128)} %convert_divide_fusion.inv_ref, f32[40]{0:T(128)} %get-tuple-element.24.root_ref, s32[1,640]{1,0:T(1,128)} %reshape.111.wave_ref, s32[1,640]{1,0:T(1,128)} %and_select_fusion.sine_ref, bf16[276,40,1408]{2,1,0:T(8,128)(2,1)} %bitcast.24), custom_call_target="tpu_custom_call" | custom-call | flops 3979345920 | bytes 9043968 | tf_op jit(solution)/shard_map/forward_cycles/pallas_call | solution.py:153
  23.6 8.3 %all-to-all-start = ((bf16[16,1,4,22,8,128]{5,4,3,2,1,0:T(8,128)(2,1)}), bf16[16,1,4,22,8,128]{5,4,3,2,1,0:T(8,128)(2,1)S(1)}, u32[]{:S(2)}, u32[]{:S(2)}) async-start(bf16[16,1,4,22,8,128]{5,4,3,2,1,0:T(8,128)(2,1)} %forward_cycles.2), calls=%async_computation | async-start | bytes 5767168 | tf_op jit(solution)/shard_map/all_to_all | solution.py:439
  32.0 55.1 %forward_cycles.3 = (bf16[16,4,2,22,8,128]{5,4,3,2,1,0:T(8,128)(2,1)}, bf16[16,4,2,22,8,128]{5,4,3,2,1,0:T(8,128)(2,1)}) custom-call(s32[40]{0:T(128)} %copy-done.4, f32[40]{0:T(128)} %convert_divide_fusion.inv_ref, f32[40]{0:T(128)} %get-tuple-element.24.root_ref, s32[1,640]{1,0:T(1,128)} %reshape.111.wave_ref, s32[1,640]{1,0:T(1,128)} %and_select_fusion.sine_ref, ...), custom_call_target="tpu_custom_call" | custom-call | flops 15917383680 | bytes 36175872 | tf_op jit(solution)/shard_map/forward_cycles/pallas_call | solution.py:153
  87.1 1.2 all-to-all-done.rest_0_
  88.3 141.0 %all_to_all.35.rest_1_ = bf16[16,4,2,22,8,128]{5,4,3,2,1,0:T(8,128)(2,1)} all-to-all(bf16[16,4,2,22,8,128]{5,4,3,2,1,0:T(8,128)(2,1)} %get-tuple-element.12), channel_id=1, replica_groups=mesh['lat'=16,'fld'=2] {'lat'}, dimensions={0} | all-to-all | bytes 11534336 | tf_op jit(solution)/shard_map/all_to_all | solution.py:439
  229.3 4.9 all-to-all-start.2
  236.0 11.2 %fusion = bf16[6400,640]{0,1:T(8,128)(2,1)} fusion(bf16[6400,640]{1,0:T(8,128)(2,1)} %bitcast.30, s32[640]{0:T(1024)S(1)} %eq.18), kind=kOutput, calls=%fused_computation.4 | convolution fusion | flops 5247795200 | bytes 16386560 | tf_op jit(solution)/shard_map/dot_general | solution.py:471
  247.1 11.9 %copy.17 = bf16[6400,640]{1,0:T(8,128)(2,1)} copy(bf16[6400,640]{0,1:T(8,128)(2,1)} %fusion) | data formatting | bytes 16384000 | tf_op jit(solution)/shard_map/convert_element_type | solution.py:476
  259.0 13.2 %copy.22 = f32[276,2,20,320]{3,0,1,2:T(8,128)} copy(f32[276,2,20,320]{3,1,2,0:T(2,128)} %bitcast.26) | data formatting | bytes 28262400 | tf_op jit(solution)/shard_map/reshape;squeeze | solution.py:480
  272.8 0.9 broadcast_in_dim.36.weight_ref
  274.3 30.7 %middle_waves.2 = (f32[10,2,276,320]{3,2,1,0:T(8,128)}, f32[1,320]{1,0:T(1,128)}, bf16[16,5,2,22,8,128]{5,4,3,2,1,0:T(8,128)(2,1)}) custom-call(s32[10]{0:T(128)} %get-tuple-element.26.wave_ref, f32[276,320]{1,0:T(8,128)} %broadcast_in_dim.36.weight_ref, f32[1,320]{1,0:T(1,128)} %broadcast_in_dim.37.before_ref, bf16[20,320,640]{2,1,0:T(8,128)(2,1)} %bitcast.22, ...), custom_call_target="tpu_custom_call" | custom-call | flops 4521984000 | bytes 17664000 | tf_op jit(solution)/shard_map/middle_waves/pallas_call | solution.py:289
  305.0 34.8 %all-to-all-done.2.rest_1_ = bf16[16,4,2,22,8,128]{5,4,3,2,1,0:T(8,128)(2,1)} async-done(((bf16[16,4,2,22,8,128]{5,4,3,2,1,0:T(8,128)(2,1)}), bf16[16,4,2,22,8,128]{5,4,3,2,1,0:T(8,128)(2,1)}, u32[]{:S(2)}, u32[]{:S(2)}) %all-to-all-start.2) | async-done | bytes 5767200 | tf_op jit(solution)/shard_map/all_to_all | solution.py:439
  339.8 30.7 %middle_waves.3 = (f32[10,2,276,320]{3,2,1,0:T(8,128)}, f32[1,320]{1,0:T(1,128)}, bf16[16,2,2,22,8,128]{5,4,3,2,1,0:T(8,128)(2,1)}, bf16[16,2,2,22,8,128]{5,4,3,...) custom-call(s32[10]{0:T(128)} %get-tuple-element.27.wave_ref, f32[276,320]{1,0:T(8,128)} %broadcast_in_dim.36.weight_ref, ...), custom_call_target="tpu_custom_call" | custom-call | flops 4521984000 | bytes 17664000 | tf_op jit(solution)/shard_map/middle_waves/pallas_call | solution.py:289
  370.4 91.9 %all_to_all.36.rest_1_ = bf16[16,2,2,22,8,128]{5,4,3,2,1,0:T(8,128)(2,1)S(1)} all-to-all(bf16[16,2,2,22,8,128]{5,4,3,2,1,0:T(8,128)(2,1)} %get-tuple-element.17), channel_id=1, replica_groups=mesh['lat'=16,'fld'=2] {'lat'}, dimensions={0} | all-to-all | bytes 5767168 | tf_op jit(solution)/shard_map/all_to_all | solution.py:439
  462.3 69.3 %all_to_all.37.rest_1_ = bf16[16,2,2,22,8,128]{5,4,3,2,1,0:T(8,128)(2,1)} all-to-all(bf16[16,2,2,22,8,128]{5,4,3,2,1,0:T(8,128)(2,1)} %get-tuple-element.20), channel_id=1, replica_groups=mesh['lat'=16,'fld'=2] {'lat'}, dimensions={0} | all-to-all | bytes 5767168 | tf_op jit(solution)/shard_map/all_to_all | solution.py:439
  531.6 161.4 %all_to_all.38.rest_0_ = bf16[16,5,2,22,8,128]{5,4,3,2,1,0:T(8,128)(2,1)} all-to-all(bf16[16,5,2,22,8,128]{5,4,3,2,1,0:T(8,128)(2,1)} %get-tuple-element.18), channel_id=1, replica_groups=mesh['lat'=16,'fld'=2] {'lat'}, dimensions={0} | all-to-all | bytes 14417920 | tf_op jit(solution)/shard_map/all_to_all | solution.py:439
  692.9 4.6 all-to-all-start.5
  699.0 6.8 maximum_bitcast_fusion
  705.8 17.9 %copy.20 = f32[276,2,20,320]{3,1,2,0:T(2,128)} copy(f32[276,2,20,320]{3,0,1,2:T(8,128)S(1)} %maximum_bitcast_fusion) | data formatting | bytes 28262400 | tf_op jit(solution)/shard_map/transpose | solution.py:505
  725.4 31.5 %backward_cycles.3.rest_2_ = bf16[276,40,1408]{2,1,0:T(8,128)(2,1)} custom-call(s32[40]{0:T(128)} %copy-done.4, f32[40]{0:T(128)} %convert_divide_fusion.inv_ref, f32[40]{0:T(128)} %get-tuple-element.24.root_ref, s32[1,640]{1,0:T(1,128)} %reshape.111.wave_ref, s32[1,640]{1,0:T(1,128)} %and_select_fusion.sine_ref, ...), custom_call_target="tpu_custom_call" | custom-call | flops 7958691840 | bytes 18087936 | tf_op jit(solution)/shard_map/backward_cycles/pallas_call | solution.py:414
  757.0 31.5 %backward_cycles.4.rest_2_ = bf16[276,40,1408]{2,1,0:T(8,128)(2,1)} custom-call(s32[40]{0:T(128)} %copy-done.4, f32[40]{0:T(128)} %convert_divide_fusion.inv_ref, f32[40]{0:T(128)} %get-tuple-element.24.root_ref, s32[1,640]{1,0:T(1,128)} %reshape.111.wave_ref, s32[1,640]{1,0:T(1,128)} %and_select_fusion.sine_ref, ...), custom_call_target="tpu_custom_call", output_to_operand_aliasing={{}: (7, {})} | custom-call | flops 7958691840 | bytes 18087936 | tf_op jit(solution)/shard_map/backward_cycles/pallas_call | solution.py:414
  788.5 18.0 %backward_cycles.5 = bf16[276,40,1408]{2,1,0:T(8,128)(2,1)} custom-call(s32[40]{0:T(128)} %copy-done.4, f32[40]{0:T(128)} %convert_divide_fusion.inv_ref, f32[40]{0:T(128)} %get-tuple-element.24.root_ref, s32[1,640]{1,0:T(1,128)} %reshape.111.wave_ref, s32[1,640]{1,0:T(1,128)} %and_select_fusion.sine_ref, ...), custom_call_target="tpu_custom_call", output_to_operand_aliasing={{}: (7, {})} | custom-call | flops 3979345920 | bytes 9043968 | tf_op jit(solution)/shard_map/backward_cycles/pallas_call | solution.py:414
  (37 shorter events, 7.6 us)
Async XLA Ops:
  0.6 1.4 copy-start
  4.1 2.1 copy-start.4
  23.6 64.7 %all-to-all-start = ((bf16[16,1,4,22,8,128]{5,4,3,2,1,0:T(8,128)(2,1)}), bf16[16,1,4,22,8,128]{5,4,3,2,1,0:T(8,128)(2,1)S(1)}, u32[]{:S(2)}, u32[]{:S(2)}) async-start(bf16[16,1,4,22,8,128]{5,4,3,2,1,0:T(8,128)(2,1)} %forward_cycles.2), calls=%async_computation | async-start | bytes 5767168 | tf_op jit(solution)/shard_map/all_to_all | solution.py:439
  88.3 141.0 %copy-start.2 = (bf16[16,1,4,22,8,128]{5,4,3,2,1,0:T(8,128)(2,1)}, bf16[16,1,4,22,8,128]{5,4,3,2,1,0:T(8,128)(2,1)S(1)}, u32[]{:S(2)}) copy-start(bf16[16,1,4,22,8,128]{5,4,3,2,1,0:T(8,128)(2,1)S(1)} %all-to-all-done.rest_0_) | copy-start | bytes 8650756
  229.3 4.9 copy-start.5
  229.3 6.4 copy-start.6
  229.3 110.5 %all-to-all-start.2 = ((bf16[16,4,2,22,8,128]{5,4,3,2,1,0:T(8,128)(2,1)}), bf16[16,4,2,22,8,128]{5,4,3,2,1,0:T(8,128)(2,1)}, u32[]{:S(2)}, u32[]{:S(2)}) async-start(bf16[16,4,2,22,8,128]{5,4,3,2,1,0:T(8,128)(2,1)} %get-tuple-element.15), calls=%async_computation.2 | async-start | bytes 11534336 | tf_op jit(solution)/shard_map/all_to_all | solution.py:439
  462.3 235.3 %copy-start.3 = (bf16[16,2,2,22,8,128]{5,4,3,2,1,0:T(8,128)(2,1)}, bf16[16,2,2,22,8,128]{5,4,3,2,1,0:T(8,128)(2,1)S(1)}, u32[]{:S(2)}) copy-start(bf16[16,2,2,22,8,128]{5,4,3,2,1,0:T(8,128)(2,1)S(1)} %all_to_all.36.rest_1_) | copy-start | bytes 8650756
  692.9 95.5 %all-to-all-start.5 = ((bf16[16,1,2,22,8,128]{5,4,3,2,1,0:T(8,128)(2,1)}), bf16[16,1,2,22,8,128]{5,4,3,2,1,0:T(8,128)(2,1)}, u32[]{:S(2)}, u32[]{:S(2)}) async-start(bf16[16,1,2,22,8,128]{5,4,3,2,1,0:T(8,128)(2,1)} %get-tuple-element.19), calls=%async_computation.5 | async-start | bytes 2883584 | tf_op jit(solution)/shard_map/all_to_all | solution.py:439
  698.9 24.7 %collective-permute-start = (f32[8,128]{1,0:T(8,128)S(1)}, f32[8,128]{1,0:T(8,128)S(1)}, u32[]{:S(2)}, u32[]{:S(2)}) collective-permute-start(f32[8,128]{1,0:T(8,128)S(1)} %broadcast_in_dim.41), channel_id=1, source_target_pairs={{0,1},{1,0},{2,3},{3,2},{4,5},{5,4},{6,7},{7,6},{8,9},{9,8},{10,11... | collective-permute-start | bytes 12296 | tf_op jit(solution)/shard_map/ppermute | solution.py:511
  788.4 18.0 %copy-start.1 = (s32[640]{0:T(1024)S(1)}, s32[640]{0:T(1024)}, u32[]{:S(2)}) copy-start(s32[640]{0:T(1024)} %param.10) | copy-start | bytes 7684
